TPU v7x, 32 devices: a whole 2x2x4 slice. The times are simulated.
32 devices in a mesh: section: 4 (over y, core), dp: 8 (over z, x).
Axes of the slice: x: 2, y: 2, z: 4, core: 2. Of those that a mesh axis runs over, the one named last changes fastest.
Arguments:
- latents: bfloat16 [16, 4, 128], P('dp'), may hold values from -6 to 6
- noise: bfloat16 [16, 4, 128], P('dp'), may hold values from -6 to 6
- timesteps: int32 [16], P('dp'), may hold values from 0 to 999
- cameras: int32 [16, 4], P('dp'), may hold values from 0 to 31
- embed_in: bfloat16 [4, 1024], replicated, may hold values from -3 to 3
- camera_table: bfloat16 [32, 1024], replicated, may hold values from -6 to 6
- w_mod: bfloat16 [4, 256, 3072], P('section'), may hold values from -0.375 to 0.375
- w_qkv: bfloat16 [4, 1024, 3072], P('section'), may hold values from -0.1875 to 0.1875
- w_out: bfloat16 [4, 1024, 1024], P('section'), may hold values from -0.1875 to 0.1875
- head_out: bfloat16 [4, 1024], replicated, may hold values from -0.1875 to 0.1875
- moment_qkv: float32 [4, 1024, 3072], P('section', 'dp'), may hold values from -6 to 6
- moment_out: float32 [4, 1024, 1024], P('section', 'dp'), may hold values from -6 to 6
- second_qkv: float32 [4, 1024, 3072], P('section', 'dp'), may hold values from 0.25 to 4
- second_out: float32 [4, 1024, 1024], P('section', 'dp'), may hold values from 0.25 to 4
Outputs:
- update_qkv: float32 [4, 1024, 3072], P('section', 'dp')
- update_out: float32 [4, 1024, 1024], P('section', 'dp')
- new_moment_qkv: float32 [4, 1024, 3072], P('section', 'dp')
- new_moment_out: float32 [4, 1024, 1024], P('section', 'dp')
- new_second_qkv: float32 [4, 1024, 3072], P('section', 'dp')
- new_second_out: float32 [4, 1024, 1024], P('section', 'dp')
All inputs are finite; a program needn't handle non-finite values.
Results may differ from a plain program's by a relative error of at most 0.00045.
Values may be sent and summed in bfloat16 or wider, within the bound.
A program may use at most 128 MiB of HBM per device.

v0:
```python
import math

import jax
import jax.numpy as jnp
from jax import lax
from jax.sharding import PartitionSpec as P

HEADS = 16
HEAD_DIM = 64


def passed_along(x, axis, by):
    devices = lax.axis_size(axis)
    pairs = [(i, i + by) for i in range(devices) if 0 <= i + by < devices]
    return lax.ppermute(x, axis, pairs)


def time_embed(step_ids, emb_width):
    half_dim = emb_width // 2
    frequency = jnp.exp(-math.log(10000.0) * jnp.arange(half_dim, dtype=jnp.float32) / half_dim)
    phases = step_ids.astype(jnp.float32)[:, None] * frequency[None, :]
    joined = jnp.concatenate([jnp.cos(phases), jnp.sin(phases)], axis=-1)
    return jax.nn.silu(joined).astype(jnp.bfloat16)


def embed_sample(latent_now, noise_now, step_now, camera_now, embed_in, camera_table):
    step_f = step_now.astype(jnp.float32)
    alpha_bar = jnp.cos((step_f / 1000.0 + 0.008) / 1.008 * (math.pi / 2.0)) ** 2
    noised = jnp.sqrt(alpha_bar) * latent_now.astype(jnp.float32) + jnp.sqrt(
        1.0 - alpha_bar
    ) * noise_now.astype(jnp.float32)
    features = lax.dot_general(
        noised.astype(jnp.bfloat16),
        embed_in,
        (((0,), (0,)), ((), ())),
        preferred_element_type=jnp.float32,
    )
    onehot = (
        camera_now[:, None] == jnp.arange(camera_table.shape[0], dtype=jnp.int32)[None, :]
    ).astype(jnp.bfloat16)
    camera_vec = jnp.dot(onehot, camera_table, preferred_element_type=jnp.float32)
    model_width = embed_in.shape[1]
    views = camera_now.shape[0]
    joined = features.reshape(views, -1, model_width) + camera_vec[:, None, :]
    return joined.reshape(-1, model_width).astype(jnp.bfloat16)


def normed_of(layer_h, shift_mod, scale_mod):
    hidden_f = layer_h.astype(jnp.float32)
    mean_sq = jnp.mean(hidden_f * hidden_f, axis=-1, keepdims=True)
    return (hidden_f * lax.rsqrt(mean_sq + 1e-06) * (1.0 + scale_mod) + shift_mod).astype(
        jnp.bfloat16
    )


def piece_a(layer_h, weight_qkv, shift_mod, scale_mod):
    normed = normed_of(layer_h, shift_mod, scale_mod)
    return jnp.dot(normed, weight_qkv, preferred_element_type=jnp.float32).astype(jnp.bfloat16)


def piece_b(qkv_rows):
    seq_len = qkv_rows.shape[0]
    model_width = qkv_rows.shape[1] // 3
    queries = qkv_rows[:, :model_width].reshape(seq_len, HEADS, HEAD_DIM)
    keys_in = qkv_rows[:, model_width : 2 * model_width].reshape(seq_len, HEADS, HEAD_DIM)
    values_in = qkv_rows[:, 2 * model_width :].reshape(seq_len, HEADS, HEAD_DIM)
    scores = jnp.einsum("qhd,khd->hqk", queries, keys_in, preferred_element_type=jnp.float32) * (
        1.0 / math.sqrt(HEAD_DIM)
    )
    probabilities = jax.nn.softmax(scores, axis=-1).astype(jnp.bfloat16)
    attended = jnp.einsum(
        "hqk,khd->qhd", probabilities, values_in, preferred_element_type=jnp.float32
    )
    return attended.reshape(seq_len, model_width).astype(jnp.bfloat16)


def piece_c(attended, layer_h, weight_out, gate_mod):
    projected = jnp.dot(attended, weight_out, preferred_element_type=jnp.float32)
    return (layer_h.astype(jnp.float32) + gate_mod * projected).astype(jnp.bfloat16)


def output_grad(final_h, head_out, noise_now):

    def squared(hidden_in):
        hidden_f = hidden_in.astype(jnp.float32)
        mean_sq = jnp.mean(hidden_f * hidden_f, axis=-1, keepdims=True)
        normed = (hidden_f * lax.rsqrt(mean_sq + 1e-06)).astype(jnp.bfloat16)
        predicted = lax.dot_general(
            head_out, normed, (((1,), (1,)), ((), ())), preferred_element_type=jnp.float32
        )
        error_val = predicted - noise_now.astype(jnp.float32)
        return jnp.sum(error_val * error_val)

    loss_val, pull_back = jax.vjp(squared, final_h)
    return pull_back(jnp.ones_like(loss_val))[0]


def optimizer_step(gradient, moment, second, factor):
    normalized = gradient * factor
    moment_new = 0.9 * moment + 0.1 * normalized
    second_new = 0.99 * second + 0.01 * normalized * normalized
    return (moment_new / (jnp.sqrt(second_new) + 1e-08), moment_new, second_new)


def pick_row(array, micro_slot):
    return lax.dynamic_index_in_dim(array, micro_slot, 0, keepdims=False)


def put_row(array, value, micro_slot):
    return lax.dynamic_update_index_in_dim(array, value, micro_slot, 0)


def local(
    latents,
    noise,
    timesteps,
    cameras,
    embed_in,
    camera_table,
    w_mod,
    w_qkv,
    w_out,
    head_out,
    moment_qkv,
    moment_out,
    second_qkv,
    second_out,
):
    sections = lax.axis_size("section")
    section_id = lax.axis_index("section")
    last_section = sections - 1
    micro_count = latents.shape[0]
    seq_len = latents.shape[2]
    model_width = w_qkv.shape[1]
    tick_count = micro_count + sections - 1
    w_qkv_layer = w_qkv[0]
    w_out_layer = w_out[0]
    time_emb = time_embed(timesteps, w_mod.shape[1])
    modulation = jnp.dot(time_emb, w_mod[0], preferred_element_type=jnp.float32)
    zero_act = jnp.zeros((seq_len, model_width), jnp.bfloat16)

    def mods_of(micro_slot):
        mod_row = pick_row(modulation, micro_slot)
        return (
            mod_row[:model_width],
            mod_row[model_width : 2 * model_width],
            mod_row[2 * model_width :],
        )

    stored_h = jnp.zeros((micro_count, seq_len, model_width), jnp.bfloat16)
    grad_final = jnp.zeros((micro_count, seq_len, model_width), jnp.bfloat16)
    stored_qkv = None
    stored_attn = None
    buffers = (stored_h, stored_qkv, stored_attn, grad_final)
    sent_act = zero_act
    for tick_num in range(tick_count):
        received = passed_along(sent_act, "section", 1) if tick_num > 0 else zero_act
        micro_index = tick_num - section_id
        is_active = (micro_index >= 0) & (micro_index < micro_count)
        micro_slot = jnp.clip(micro_index, 0, micro_count - 1)
        noise_now = pick_row(noise, micro_slot)
        embedded = embed_sample(
            pick_row(latents, micro_slot),
            noise_now,
            pick_row(timesteps, micro_slot),
            pick_row(cameras, micro_slot),
            embed_in,
            camera_table,
        )
        layer_in = jnp.where(section_id == 0, embedded, received)
        shift_mod, scale_mod, gate_mod = mods_of(micro_slot)

        def active(
            state,
            layer_in=layer_in,
            noise_now=noise_now,
            micro_slot=micro_slot,
            shift_mod=shift_mod,
            scale_mod=scale_mod,
            gate_mod=gate_mod,
        ):
            held_h, held_qkv, held_attn, held_grad = state
            qkv_rows = piece_a(layer_in, w_qkv_layer, shift_mod, scale_mod)
            attended = piece_b(qkv_rows)
            layer_out = piece_c(attended, layer_in, w_out_layer, gate_mod)
            head_grad = lax.cond(
                section_id == last_section,
                lambda final_h: output_grad(final_h, head_out, noise_now),
                lambda final_h: jnp.zeros_like(final_h),
                layer_out,
            )
            held_h = put_row(held_h, layer_in, micro_slot)
            held_grad = put_row(held_grad, head_grad, micro_slot)
            return (layer_out, (held_h, held_qkv, held_attn, held_grad))

        def resting(state):
            return (zero_act, state)

        sent_act, buffers = lax.cond(is_active, active, resting, buffers)
    stored_h, stored_qkv, stored_attn, grad_final = buffers
    cot_qkv = jnp.zeros((micro_count, seq_len, 3 * model_width), jnp.bfloat16)
    cot_proj = jnp.zeros((micro_count, seq_len, model_width), jnp.bfloat16)
    back_attn = jnp.zeros((micro_count, seq_len, model_width), jnp.bfloat16)
    back_state = (cot_qkv, cot_proj, back_attn)
    sent_grad = zero_act
    for tick_num in range(tick_count):
        received = passed_along(sent_grad, "section", -1) if tick_num > 0 else zero_act
        micro_index = tick_num - (last_section - section_id)
        is_active = (micro_index >= 0) & (micro_index < micro_count)
        micro_slot = jnp.clip(micro_index, 0, micro_count - 1)
        grad_out = jnp.where(section_id == last_section, pick_row(grad_final, micro_slot), received)
        layer_in = pick_row(stored_h, micro_slot)
        shift_mod, scale_mod, gate_mod = mods_of(micro_slot)

        def backward(
            state,
            layer_in=layer_in,
            grad_out=grad_out,
            micro_slot=micro_slot,
            shift_mod=shift_mod,
            scale_mod=scale_mod,
            gate_mod=gate_mod,
        ):
            held_cot_qkv, held_cot_proj, held_attn = state
            qkv_rows = piece_a(layer_in, w_qkv_layer, shift_mod, scale_mod)
            attended = piece_b(qkv_rows)
            held_attn = put_row(held_attn, attended, micro_slot)
            _, pull_c = jax.vjp(
                lambda attn_in, hidden_in: piece_c(attn_in, hidden_in, w_out_layer, gate_mod),
                attended,
                layer_in,
            )
            grad_attn, grad_res = pull_c(grad_out)
            proj_cot = (gate_mod * grad_out.astype(jnp.float32)).astype(jnp.bfloat16)
            _, pull_b = jax.vjp(piece_b, qkv_rows)
            grad_qkv_rows = pull_b(grad_attn)[0]
            _, pull_a = jax.vjp(
                lambda hidden_in: piece_a(hidden_in, w_qkv_layer, shift_mod, scale_mod), layer_in
            )
            grad_hidden = pull_a(grad_qkv_rows)[0]
            grad_total = (grad_hidden.astype(jnp.float32) + grad_res.astype(jnp.float32)).astype(
                jnp.bfloat16
            )
            held_cot_qkv = put_row(held_cot_qkv, grad_qkv_rows, micro_slot)
            held_cot_proj = put_row(held_cot_proj, proj_cot, micro_slot)
            return (grad_total, (held_cot_qkv, held_cot_proj, held_attn))

        def waiting(state):
            return (zero_act, state)

        sent_grad, back_state = lax.cond(is_active, backward, waiting, back_state)
    cot_qkv, cot_proj, back_attn = back_state
    shift_all = modulation[:, None, :model_width]
    scale_all = modulation[:, None, model_width : 2 * model_width]
    rows_all = micro_count * seq_len
    normed_all = normed_of(stored_h, shift_all, scale_all).reshape(rows_all, model_width)
    qkv_shard = lax.psum_scatter(
        lax.dot_general(
            normed_all,
            cot_qkv.reshape(rows_all, 3 * model_width),
            (((0,), (0,)), ((), ())),
            preferred_element_type=jnp.float32,
        )[None],
        "dp",
        scatter_dimension=1,
        tiled=True,
    )
    out_shard = lax.psum_scatter(
        lax.dot_general(
            back_attn.reshape(rows_all, model_width),
            cot_proj.reshape(rows_all, model_width),
            (((0,), (0,)), ((), ())),
            preferred_element_type=jnp.float32,
        )[None],
        "dp",
        scatter_dimension=1,
        tiled=True,
    )
    local_sq = jnp.sum(qkv_shard * qkv_shard) + jnp.sum(out_shard * out_shard)
    total_sq = lax.psum(local_sq, ("section", "dp"))
    factor = lax.rsqrt(total_sq / (sections * 4 * model_width * model_width) + 1e-12)
    update_qkv, new_moment_qkv, new_second_qkv = optimizer_step(
        qkv_shard, moment_qkv, second_qkv, factor
    )
    update_out, new_moment_out, new_second_out = optimizer_step(
        out_shard, moment_out, second_out, factor
    )
    return (update_qkv, update_out, new_moment_qkv, new_moment_out, new_second_qkv, new_second_out)


def solution(mesh):
    placed = (
        P("dp", None, None),
        P("dp", None, None),
        P("dp"),
        P("dp", None),
        P(),
        P(),
        P("section", None, None),
        P("section", None, None),
        P("section", None, None),
        P(),
        P("section", "dp", None),
        P("section", "dp", None),
        P("section", "dp", None),
        P("section", "dp", None),
    )
    return jax.shard_map(
        local,
        mesh=mesh,
        in_specs=placed,
        out_specs=(
            P("section", "dp", None),
            P("section", "dp", None),
            P("section", "dp", None),
            P("section", "dp", None),
            P("section", "dp", None),
            P("section", "dp", None),
        ),
        check_vma=False,
    )
```

profile of v0, /device:TPU:0, one launch (start us, length us, event | category | flops | bytes accessed | tf_op | source)
XLA Modules:
  0.0 563.7 jit_solution(17396369308295830882)
XLA Ops:
  18.8 10.8 %conditional.21 = (bf16[128,1024]{1,0:T(8,128)(2,1)}, bf16[2,128,1024]{2,1,0:T(8,128)(2,1)S(1)}, bf16[2,128,1024]{2,1,0:T(8,128)(2,1)}) conditional(s32[]{:T(128)} %convert_element_type.1107, () %tuple.178, (f32[4,1024]{1,0:T(4,128)S(1)}, f32[4,32,1024]{2,1,0:T(8,128)S(1)}, pred[128,1024]{1,0:T(8,128)(4,1)S(1)}, bf16[128,1024]{1,0:T(8,128)(2,1)S(1)}, ...), branch_computations={%region_0.1_spmd, %region_1.9_spmd} | conditional | flops 1183061632 | bytes 27218128 | solution.py:199
  19.3 4.0 convolution_convert_fusion.1
  25.2 2.8 fusion.18
  32.3 9.7 %conditional.22 = (bf16[128,1024]{1,0:T(8,128)(2,1)}, bf16[2,128,1024]{2,1,0:T(8,128)(2,1)S(1)}, bf16[2,128,1024]{2,1,0:T(8,128)(2,1)}) conditional(s32[]{:T(128)} %convert_element_type.1106, (bf16[2,128,1024]{2,1,0:T(8,128)(2,1)S(1)}, bf16[2,128,1024]{2,1,0:T(8,128)(2,1)}) %tuple.180, (f32[4,1024]{1,0:T(4,128)S(1)}, f32[4,32,1024]{2,1,0:T(8,128)S(1)}, ...), branch_computations={%region_9.10_spmd, %region_10.18_spmd} | conditional | flops 1183061632 | bytes 21975180 | solution.py:199
  32.7 3.9 convolution_convert_fusion.4
  38.4 2.8 fusion.47
  41.9 2.3 collective-permute-start.1
  45.6 7.5 %conditional.23 = (bf16[128,1024]{1,0:T(8,128)(2,1)}, bf16[2,128,1024]{2,1,0:T(8,128)(2,1)S(1)}, bf16[2,128,1024]{2,1,0:T(8,128)(2,1)}) conditional(s32[]{:T(128)} %convert_element_type.1105, (bf16[2,128,1024]{2,1,0:T(8,128)(2,1)S(1)}, bf16[2,128,1024]{2,1,0:T(8,128)(2,1)}) %tuple.182, (f32[4,1024]{1,0:T(4,128)S(1)}, ...), branch_computations={%region_18.19_spmd, %region_19.27_spmd} | conditional | flops 1183061632 | bytes 21975180 | solution.py:199
  53.1 7.0 %collective-permute-start.2 = (bf16[128,1024]{1,0:T(8,128)(2,1)}, bf16[128,1024]{1,0:T(8,128)(2,1)S(1)}, u32[]{:S(2)}, u32[]{:S(2)}) collective-permute-start(bf16[128,1024]{1,0:T(8,128)(2,1)} %get-tuple-element.1274), channel_id=1, source_target_pairs={{0,8},{8,16},{16,24},{1,9},{9,17},{17,25},{2,10},{10,18},{18,26},{... | collective-permute-start | bytes 786440 | tf_op jit(solution)/shard_map/ppermute | solution.py:15
  62.2 6.5 %collective-permute-start.3 = (bf16[128,1024]{1,0:T(8,128)(2,1)}, bf16[128,1024]{1,0:T(8,128)(2,1)S(1)}, u32[]{:S(2)}, u32[]{:S(2)}) collective-permute-start(bf16[128,1024]{1,0:T(8,128)(2,1)} %get-tuple-element.1277), channel_id=1, source_target_pairs={{0,8},{8,16},{16,24},{1,9},{9,17},{17,25},{2,10},{10,18},{18,26},{... | collective-permute-start | bytes 786440 | tf_op jit(solution)/shard_map/ppermute | solution.py:15
  70.3 1.7 conditional.26
  73.3 15.2 %collective-permute-done.4 = bf16[128,1024]{1,0:T(8,128)(2,1)S(1)} collective-permute-done((bf16[128,1024]{1,0:T(8,128)(2,1)S(1)}, bf16[128,1024]{1,0:T(8,128)(2,1)S(1)}, u32[]{:S(2)}, u32[]{:S(2)}) %collective-permute-start.4) | collective-permute-done | bytes 262176 | tf_op jit(solution)/shard_map/ppermute | solution.py:15
  91.1 7.2 %collective-permute-done.5 = bf16[128,1024]{1,0:T(8,128)(2,1)S(1)} collective-permute-done((bf16[128,1024]{1,0:T(8,128)(2,1)}, bf16[128,1024]{1,0:T(8,128)(2,1)S(1)}, u32[]{:S(2)}, u32[]{:S(2)}) %collective-permute-start.5) | collective-permute-done | bytes 262176 | tf_op jit(solution)/shard_map/ppermute | solution.py:15
  100.8 62.0 %collective-permute-done.6 = bf16[128,1024]{1,0:T(8,128)(2,1)S(1)} collective-permute-done((bf16[128,1024]{1,0:T(8,128)(2,1)}, bf16[128,1024]{1,0:T(8,128)(2,1)S(1)}, u32[]{:S(2)}, u32[]{:S(2)}) %collective-permute-start.6) | collective-permute-done | bytes 262176 | tf_op jit(solution)/shard_map/ppermute | solution.py:15
  162.7 19.2 %conditional.29 = (bf16[128,1024]{1,0:T(8,128)(2,1)}, bf16[2,128,3072]{1,2,0:T(8,128)(2,1)}, bf16[2,128,1024]{2,1,0:T(8,128)(2,1)S(1)}, bf16[2,128,1024]{1,2,0:T(8,128)(2,1)S(1)}) conditional(s32[]{:T(128)} %convert_element_type.1133, (bf16[2,128,3072]{1,2,0:T(8,128)(2,1)}, bf16[2,128,1024]{2,1,0:T(8,128)(2,1)S(1)}, ...), branch_computations={%region_67.68_spmd, %region_68.74_spmd} | conditional | flops 2095847296 | bytes 64775476 | solution.py:251
  164.2 2.4 convolution_convert_fusion.44
  166.9 3.9 convolution_convert_fusion.37
  172.8 1.6 convolution_convert_fusion.39
  178.7 2.3 fusion.249
  183.2 6.6 %collective-permute-done.7 = bf16[128,1024]{1,0:T(8,128)(2,1)S(1)} collective-permute-done((bf16[128,1024]{1,0:T(8,128)(2,1)}, bf16[128,1024]{1,0:T(8,128)(2,1)S(1)}, u32[]{:S(2)}, u32[]{:S(2)}) %collective-permute-start.7) | collective-permute-done | bytes 262176 | tf_op jit(solution)/shard_map/ppermute | solution.py:15
  189.8 14.3 %conditional.30 = ((bf16[2,128,3072]{1,2,0:T(8,128)(2,1)}, bf16[2,128,1024]{2,1,0:T(8,128)(2,1)S(1)}, bf16[2,128,1024]{1,2,0:T(8,128)(2,1)S(1)})) conditional(s32[]{:T(128)} %convert_element_type.1132, (bf16[2,128,3072]{1,2,0:T(8,128)(2,1)}, bf16[2,128,1024]{2,1,0:T(8,128)(2,1)S(1)}, bf16[2,128,1024]{1,2,0:T(8,128)(2,1)S(1)}) %tuple.196, ...), branch_computations={%region_74.75_spmd, %region_75.80_spmd} | conditional | flops 1286214912 | bytes 32655504 | solution.py:251
  191.1 2.5 convolution_convert_fusion.51
  193.8 3.9 convolution_convert_fusion.45
  199.8 1.6 convolution_convert_fusion.47
  204.1 2.7 convolution_bitcast_fusion.6
  207.1 8.0 %convolution_bitcast_fusion.5 = f32[1,1024,3072]{2,1,0:T(8,128)} fusion(bf16[2,128,3072]{1,2,0:T(8,128)(2,1)} %get-tuple-element.1296, bf16[2,128,1024]{2,1,0:T(8,128)(2,1)S(1)} %get-tuple-element.1335, f32[2,1024]{1,0:T(2,128)S(1)} %get-tuple-element.1488, f32[2,1024]{1,0:T(2,128)S(1)} %get-tuple-element.1487, f32[2,128]{1,0:T(2,128)S(1)} %add_rsqrt_fusion.6), kind=kOutput, calls=%fused_computation.524 | convolution fusion | flops 1611923456 | bytes 14697472 | tf_op jit(solution)/shard_map/dot_general | solution.py:258
  215.1 81.9 %reduce-scatter.5.cloned.1.call-done = f32[1,128,1024]{2,1,0:T(8,128)} async-done(((f32[1,1024,1024]{2,1,0:T(8,128)}), f32[1,128,1024]{2,1,0:T(8,128)}) %reduce-scatter.5.cloned.1.call-update) | async-done | bytes 524304 | tf_op jit(solution)/shard_map/reduce_scatter | solution.py:268
  297.0 1.9 multiply_reduce_fusion.3
  299.0 208.8 %reduce-scatter.3.cloned.1.call-done = f32[1,128,3072]{2,1,0:T(8,128)} async-done(((f32[1,1024,3072]{2,1,0:T(8,128)}), f32[1,128,3072]{2,1,0:T(8,128)}) %reduce-scatter.3.cloned.1.call-update) | async-done | bytes 1572880 | tf_op jit(solution)/shard_map/reduce_scatter | solution.py:257
  507.7 2.4 multiply_reduce_fusion.2
  511.5 39.3 %psum.7 = f32[]{:T(128)} all-reduce(f32[]{:T(128)S(6)} %add.744), channel_id=1, replica_groups=mesh['section'=4,'dp'=8] {'section','dp'}, use_global_device_ids=true, to_apply=%region_84.85 | all-reduce | flops 1 | bytes 8 | tf_op jit(solution)/shard_map/psum | solution.py:280
  553.9 2.7 add_divide_fusion
  (168 shorter events, 51.9 us)
Async XLA Ops:
  7.2 11.2 %copy-start = (bf16[1,256,3072]{2,1,0:T(8,128)(2,1)S(1)}, bf16[1,256,3072]{2,1,0:T(8,128)(2,1)}, u32[]{:S(2)}) copy-start(bf16[1,256,3072]{2,1,0:T(8,128)(2,1)} %param.50) | copy-start | bytes 4718596
  7.2 11.6 %copy-start.18 = (bf16[4,1024]{1,0:T(4,128)(2,1)S(1)}, bf16[4,1024]{1,0:T(4,128)(2,1)}, u32[]{:S(2)}) copy-start(bf16[4,1024]{1,0:T(4,128)(2,1)} %param.53) | copy-start | bytes 24580
  7.2 289.8 %reduce-scatter.5.cloned.1.call-start = ((), (), s32[]{:S(2)}) async-start(), calls=%async_computation.3 | async-start | bytes 4718592 | tf_op jit(solution)/shard_map/reduce_scatter | solution.py:268
  18.8 12.2 %copy-start.32 = (bf16[32,1024]{1,0:T(8,128)(2,1)S(1)}, bf16[32,1024]{1,0:T(8,128)(2,1)}, u32[]{:S(2)}) copy-start(bf16[32,1024]{1,0:T(8,128)(2,1)} %param.49) | copy-start | bytes 196612
  18.8 12.4 %copy-start.31 = (bf16[4,1024]{1,0:T(4,128)(2,1)S(1)}, bf16[4,1024]{1,0:T(4,128)(2,1)}, u32[]{:S(2)}) copy-start(bf16[4,1024]{1,0:T(4,128)(2,1)} %param.48) | copy-start | bytes 24580
  19.3 4.1 copy-start.2
  28.0 1.6 copy-start.3
  29.6 2.6 collective-permute-start
  41.9 3.6 collective-permute-start.1
  53.1 8.4 %collective-permute-start.2 = (bf16[128,1024]{1,0:T(8,128)(2,1)}, bf16[128,1024]{1,0:T(8,128)(2,1)S(1)}, u32[]{:S(2)}, u32[]{:S(2)}) collective-permute-start(bf16[128,1024]{1,0:T(8,128)(2,1)} %get-tuple-element.1274), channel_id=1, source_target_pairs={{0,8},{8,16},{16,24},{1,9},{9,17},{17,25},{2,10},{10,18},{18,26},{... | collective-permute-start | bytes 786440 | tf_op jit(solution)/shard_map/ppermute | solution.py:15
  62.2 7.9 %collective-permute-start.3 = (bf16[128,1024]{1,0:T(8,128)(2,1)}, bf16[128,1024]{1,0:T(8,128)(2,1)S(1)}, u32[]{:S(2)}, u32[]{:S(2)}) collective-permute-start(bf16[128,1024]{1,0:T(8,128)(2,1)} %get-tuple-element.1277), channel_id=1, source_target_pairs={{0,8},{8,16},{16,24},{1,9},{9,17},{17,25},{2,10},{10,18},{18,26},{... | collective-permute-start | bytes 786440 | tf_op jit(solution)/shard_map/ppermute | solution.py:15
  72.0 16.5 %collective-permute-start.4 = (bf16[128,1024]{1,0:T(8,128)(2,1)S(1)}, bf16[128,1024]{1,0:T(8,128)(2,1)S(1)}, u32[]{:S(2)}, u32[]{:S(2)}) collective-permute-start(bf16[128,1024]{1,0:T(8,128)(2,1)S(1)} %get-tuple-element.1283), channel_id=1, source_target_pairs={{8,0},{16,8},{24,16},{9,1},{17,9},{25,17},{10,2},{18,10},{26,18},{... | collective-permute-start | bytes 786440 | tf_op jit(solution)/shard_map/ppermute | solution.py:15
  89.8 8.5 %collective-permute-start.5 = (bf16[128,1024]{1,0:T(8,128)(2,1)}, bf16[128,1024]{1,0:T(8,128)(2,1)S(1)}, u32[]{:S(2)}, u32[]{:S(2)}) collective-permute-start(bf16[128,1024]{1,0:T(8,128)(2,1)} %get-tuple-element.1287), channel_id=1, source_target_pairs={{8,0},{16,8},{24,16},{9,1},{17,9},{25,17},{10,2},{18,10},{26,18},{... | collective-permute-start | bytes 786440 | tf_op jit(solution)/shard_map/ppermute | solution.py:15
  99.5 63.3 %collective-permute-start.6 = (bf16[128,1024]{1,0:T(8,128)(2,1)}, bf16[128,1024]{1,0:T(8,128)(2,1)S(1)}, u32[]{:S(2)}, u32[]{:S(2)}) collective-permute-start(bf16[128,1024]{1,0:T(8,128)(2,1)} %get-tuple-element.1291), channel_id=1, source_target_pairs={{8,0},{16,8},{24,16},{9,1},{17,9},{25,17},{10,2},{18,10},{26,18},{... | collective-permute-start | bytes 786440 | tf_op jit(solution)/shard_map/ppermute | solution.py:15
  171.1 1.7 copy-start.27
  171.3 3.1 copy-start.29
  172.8 1.7 copy-start.16
  175.0 1.0 copy-start.28
  175.0 3.7 slice-start.6
  175.9 1.3 copy-start.30
  175.9 2.8 slice-start.7
  181.9 7.9 %collective-permute-start.7 = (bf16[128,1024]{1,0:T(8,128)(2,1)}, bf16[128,1024]{1,0:T(8,128)(2,1)S(1)}, u32[]{:S(2)}, u32[]{:S(2)}) collective-permute-start(bf16[128,1024]{1,0:T(8,128)(2,1)} %get-tuple-element.1295), channel_id=1, source_target_pairs={{8,0},{16,8},{24,16},{9,1},{17,9},{25,17},{10,2},{18,10},{26,18},{... | collective-permute-start | bytes 786440 | tf_op jit(solution)/shard_map/ppermute | solution.py:15
  199.8 1.7 copy-start.17
  206.8 301.0 %reduce-scatter.3.cloned.1.call-start = ((), (), s32[]{:S(2)}) async-start(), calls=%async_computation.2 | async-start | bytes 14155776 | tf_op jit(solution)/shard_map/reduce_scatter | solution.py:257
  215.1 336.4 %copy-start.19 = (f32[1,128,1024]{2,1,0:T(8,128)S(1)}, f32[1,128,1024]{2,1,0:T(8,128)}, u32[]{:S(2)}) copy-start(f32[1,128,1024]{2,1,0:T(8,128)} %param.57) | copy-start | bytes 1572868
  215.1 336.4 %copy-start.20 = (f32[1,128,1024]{2,1,0:T(8,128)S(1)}, f32[1,128,1024]{2,1,0:T(8,128)}, u32[]{:S(2)}) copy-start(f32[1,128,1024]{2,1,0:T(8,128)} %param.55) | copy-start | bytes 1572868
  297.0 254.4 %copy-start.11 = (f32[1,128,1024]{2,1,0:T(8,128)S(1)}, f32[1,128,1024]{2,1,0:T(8,128)}, u32[]{:S(2)}) copy-start(f32[1,128,1024]{2,1,0:T(8,128)} %reduce-scatter.5.cloned.1.call-done) | copy-start | bytes 1572868
  297.0 255.8 %copy-start.13 = (f32[1,128,3072]{2,1,0:T(8,128)S(1)}, f32[1,128,3072]{2,1,0:T(8,128)}, u32[]{:S(2)}) copy-start(f32[1,128,3072]{2,1,0:T(8,128)} %param.54) | copy-start | bytes 4718596
  551.5 2.0 copy-start.4
  551.5 2.4 copy-start.12
  553.9 2.7 copy-start.1
Sparse Core Ops, SparseCore 0:
  206.9 90.0 reduce-scatter.4
  300.6 207.0 reduce-scatter.2
where the time goes:
time: 572 us; the launch traced here: 564 us
  waiting for transfers between devices  385 us (67%)
  matrix products  55.3 us (10%)
  blocking collectives  39.3 us (7%)
  starting transfers between devices  22.6 us (4%)
  between operations  20.7 us (4%)
  other arithmetic  16.5 us (3%)
  local copies, waits for them, and re-layouts  16.2 us (3%)
  loops' own time  8.32 us (1%)
    reduce_scatter x1, waiting for transfers between devices, local(): lax.psum_scatter(lax.dot_general(normed_all, cot_qkv.reshape(rows_all, 3...  209 us
    ppermute x8, waiting for transfers between devices, passed_along(): return lax.ppermute(x, axis, pairs)  94.1 us
    reduce_scatter x1, waiting for transfers between devices, local(): lax.psum_scatter(lax.dot_general(back_attn.reshape(rows_all, model_width)...  81.9 us
    psum x1, blocking collectives, local(): total_sq = lax.psum(local_sq, ('section', 'dp'))  39.3 us
    ppermute x8, starting transfers between devices, passed_along(): return lax.ppermute(x, axis, pairs)  22.3 us
    dot_general x5, matrix products, piece_a(): jnp.dot(normed, weight_qkv, preferred_element_type=jnp.float32)  17.9 us
  transfers between devices with their start and end apart: 10, of which 10 were waited for; matrix products, arithmetic and copies ran while one was open for 2% of the time, Pallas kernels for 0%

commit v1 on v0

v1 whole, which is shorter than its diff:
```python
import functools
import math

import jax
import jax.numpy as jnp
from jax import lax
from jax.experimental import pallas as pl
from jax.experimental.pallas import tpu as pltpu
from jax.sharding import PartitionSpec as P

HEADS = 16
HEAD_DIM = 64


def time_embed(step_ids, emb_width):
    half_dim = emb_width // 2
    frequency = jnp.exp(-math.log(10000.0) * jnp.arange(half_dim, dtype=jnp.float32) / half_dim)
    phases = step_ids.astype(jnp.float32)[:, None] * frequency[None, :]
    joined = jnp.concatenate([jnp.cos(phases), jnp.sin(phases)], axis=-1)
    return jax.nn.silu(joined).astype(jnp.bfloat16)


def embed_sample(latent_now, noise_now, step_now, camera_now, embed_in, camera_table):
    step_f = step_now.astype(jnp.float32)
    alpha_bar = jnp.cos((step_f / 1000.0 + 0.008) / 1.008 * (math.pi / 2.0)) ** 2
    noised = jnp.sqrt(alpha_bar) * latent_now.astype(jnp.float32) + jnp.sqrt(
        1.0 - alpha_bar
    ) * noise_now.astype(jnp.float32)
    features = lax.dot_general(
        noised.astype(jnp.bfloat16),
        embed_in,
        (((0,), (0,)), ((), ())),
        preferred_element_type=jnp.float32,
    )
    onehot = (
        camera_now[:, None] == jnp.arange(camera_table.shape[0], dtype=jnp.int32)[None, :]
    ).astype(jnp.bfloat16)
    camera_vec = jnp.dot(onehot, camera_table, preferred_element_type=jnp.float32)
    model_width = embed_in.shape[1]
    views = camera_now.shape[0]
    joined = features.reshape(views, -1, model_width) + camera_vec[:, None, :]
    return joined.reshape(-1, model_width).astype(jnp.bfloat16)


MESH = pl.DeviceIdType.MESH
F32 = jnp.float32
BF16 = jnp.bfloat16
NT = (((1,), (1,)), ((), ()))


def dot(a, b):
    return jnp.dot(a, b, preferred_element_type=F32)


def dot_nt(a, b):
    return lax.dot_general(a, b, NT, preferred_element_type=F32)


def lane_masks():
    lane = lax.broadcasted_iota(jnp.int32, (1, 2 * HEAD_DIM), 1)
    low = jnp.where(lane < HEAD_DIM, 1.0, 0.0)
    return low.astype(BF16), (1.0 - low).astype(BF16)


def stacked(x, masks):
    return jnp.concatenate([x * masks[0], x * masks[1]], axis=0)


def step_kernel(
    h0_ref, mod_ref, noise_ref, head_ref, wqkv_hbm, wout_hbm,
    gqkv_ref, gout_ref, total_ref,
    wqkv, wout, h_in, h_recv, h_out, g_recv, g_send, nrm, qkv, att, datt, probs,
    n_own, a_own, n_par, a_par, c_own, c_par, z_send, z_recv,
    sq_own, sq_recv, sq_mid, sq_sec,
    w_sem, fwd_sem, bwd_sem, t_sem, c_sem, zs_sem, zr_sem, qs_sem, qr_sem, ss_sem, sr_sem,
):
    sections = lax.axis_size("section")
    ranks = lax.axis_size("dp")
    sec = lax.axis_index("section")
    me = lax.axis_index("dp")
    partner = me + 1 - 2 * lax.rem(me, 2)
    half = ranks // 2
    rows, width = h_in.shape
    micro = mod_ref.shape[0]
    seq = rows // micro
    share = width // ranks
    pairs = width // (2 * HEAD_DIM)

    load_qkv = pltpu.make_async_copy(wqkv_hbm, wqkv, w_sem.at[0])
    load_out = pltpu.make_async_copy(wout_hbm, wout, w_sem.at[1])
    load_qkv.start()
    load_out.start()

    barrier = pltpu.get_barrier_semaphore()

    def greet_rank(o, carry):
        pl.semaphore_signal(
            barrier, inc=1, device_id={"dp": lax.rem(me + o, ranks)}, device_id_type=MESH
        )
        return carry

    def greet_section(o, carry):
        pl.semaphore_signal(
            barrier, inc=1, device_id={"section": lax.rem(sec + o, sections)}, device_id_type=MESH
        )
        return carry

    lax.fori_loop(1, ranks, greet_rank, 0)
    lax.fori_loop(1, sections, greet_section, 0)
    pl.semaphore_wait(barrier, ranks - 1 + sections - 1)

    def remote(src, dst, send, recv, device):
        return pltpu.make_async_remote_copy(
            src_ref=src, dst_ref=dst, send_sem=send, recv_sem=recv,
            device_id=device, device_id_type=MESH,
        )

    forward = remote(
        h_out, h_recv, fwd_sem.at[0], fwd_sem.at[1],
        {"section": jnp.minimum(sec + 1, sections - 1)},
    )
    back = remote(
        g_send, g_recv, bwd_sem.at[0], bwd_sem.at[1], {"section": jnp.maximum(sec - 1, 0)}
    )
    swap_n = remote(n_own, n_par, t_sem.at[0], t_sem.at[1], {"dp": partner})
    swap_a = remote(a_own, a_par, t_sem.at[2], t_sem.at[3], {"dp": partner})
    swap_c = [
        remote(c_own.at[b], c_par.at[b], c_sem.at[0, b], c_sem.at[1, b], {"dp": partner})
        for b in range(4)
    ]

    def sample(s):
        return pl.ds(s * seq, seq)

    def mod_part(s, part):
        return mod_ref[pl.ds(s, 1), pl.ds(part * width, width)]

    @pl.when(sec == 0)
    def _():
        h_in[...] = h0_ref[...]

    @pl.when(sec > 0)
    def _():
        forward.wait_recv()
        h_in[...] = h_recv[...]

    for s in range(micro):
        h = h_in[sample(s), :].astype(F32)
        mean_sq = jnp.mean(h * h, axis=-1, keepdims=True)
        nrm[sample(s), :] = (
            h * lax.rsqrt(mean_sq + 1e-06) * (1.0 + mod_part(s, 1)) + mod_part(s, 0)
        ).astype(BF16)
    load_qkv.wait()
    tile = width // 2

    def qkv_tile(t, carry):
        cols = pl.ds(pl.multiple_of(t * tile, tile), tile)
        qkv[:, cols] = dot(nrm[...], wqkv[:, cols]).astype(BF16)
        return carry

    lax.fori_loop(0, 3 * width // tile, qkv_tile, 0)

    def heads_at(j, part):
        start = part * width + j * 2 * HEAD_DIM
        return pl.ds(pl.multiple_of(start, 2 * HEAD_DIM), 2 * HEAD_DIM)

    def attend(j, carry):
        masks = lane_masks()
        for s in range(micro):
            q2 = stacked(qkv[sample(s), heads_at(j, 0)], masks)
            k = qkv[sample(s), heads_at(j, 1)]
            v2 = stacked(qkv[sample(s), heads_at(j, 2)], masks)
            scores = dot_nt(q2, k) * (1.0 / math.sqrt(HEAD_DIM))
            e = jnp.exp(scores - jnp.max(scores, axis=-1, keepdims=True))
            p = e / jnp.sum(e, axis=-1, keepdims=True)
            probs[s * pairs + j] = p
            p2 = p.astype(BF16)
            wide = jnp.concatenate([p2[:seq], p2[seq:]], axis=1)
            att[sample(s), heads_at(j, 0)] = dot(wide, v2).astype(BF16)
        return carry

    lax.fori_loop(0, pairs, attend, 0, unroll=2)
    load_out.wait()
    otile = width // 4

    def out_tile(t, carry):
        cols = pl.ds(pl.multiple_of(t * otile, otile), otile)
        projected = dot(att[...], wout[:, cols])
        for s in range(micro):
            gate = mod_ref[pl.ds(s, 1), pl.ds(pl.multiple_of(2 * width + t * otile, otile), otile)]
            h = h_in[sample(s), cols].astype(F32)
            h_out[sample(s), cols] = (
                h + gate * projected[s * seq : (s + 1) * seq]
            ).astype(BF16)
        return carry

    lax.fori_loop(0, width // otile, out_tile, 0)

    @pl.when(sec < sections - 1)
    def _():
        forward.start()

    def turn(t, carry):
        cols = pl.ds(pl.multiple_of(t * otile, otile), otile)
        n_own[cols, :] = nrm[:, cols].T
        a_own[cols, :] = att[:, cols].T
        return carry

    lax.fori_loop(0, width // otile, turn, 0)
    swap_n.start()
    swap_a.start()

    @pl.when(sec == sections - 1)
    def _():
        for s in range(micro):
            h = h_out[sample(s), :].astype(F32)
            r = lax.rsqrt(jnp.mean(h * h, axis=-1, keepdims=True) + 1e-06)
            n = (h * r).astype(BF16)
            predicted = dot_nt(head_ref[...], n)
            err = 2.0 * (predicted - noise_ref[s])
            dn = dot(err.T.astype(BF16), head_ref[...]).astype(BF16).astype(F32)
            dh = r * dn - h * (r * r * r) * jnp.mean(dn * h, axis=-1, keepdims=True)
            g_recv[sample(s), :] = dh.astype(BF16)

    @pl.when(sec < sections - 1)
    def _():
        back.wait_recv()

    for s in range(micro):
        c_own[0, sample(s), :] = (
            mod_part(s, 2) * g_recv[sample(s), :].astype(F32)
        ).astype(BF16)
    swap_c[0].start()

    def datt_tile(t, carry):
        cols = pl.ds(pl.multiple_of(t * otile, otile), otile)
        datt[:, cols] = dot_nt(c_own[0], wout[cols, :]).astype(BF16)
        return carry

    lax.fori_loop(0, width // otile, datt_tile, 0)

    def attend_back(j, carry):
        masks = lane_masks()
        for s in range(micro):
            q2 = stacked(qkv[sample(s), heads_at(j, 0)], masks)
            k2 = stacked(qkv[sample(s), heads_at(j, 1)], masks)
            v = qkv[sample(s), heads_at(j, 2)]
            da2 = stacked(datt[sample(s), heads_at(j, 0)], masks)
            p = probs[s * pairs + j]
            dp = dot_nt(da2, v).astype(BF16).astype(F32)
            ds = (p * (dp - jnp.sum(dp * p, axis=-1, keepdims=True))) * (
                1.0 / math.sqrt(HEAD_DIM)
            )
            db = ds.astype(BF16)
            wide = jnp.concatenate([db[:seq], db[seq:]], axis=1)
            c_own[1, sample(s), heads_at(j, 0)] = dot(wide, k2).astype(BF16)
            c_own[2, sample(s), heads_at(j, 0)] = dot(ds.T.astype(BF16), q2).astype(BF16)
            c_own[3, sample(s), heads_at(j, 0)] = dot(p.T.astype(BF16), da2).astype(BF16)
        return carry

    lax.fori_loop(0, pairs, attend_back, 0, unroll=2)
    for b in range(1, 4):
        swap_c[b].start()

    @pl.when(sec > 0)
    def _():
        def dn_tile(t, carry):
            cols = pl.ds(pl.multiple_of(t * otile, otile), otile)
            datt[:, cols] = (
                dot_nt(c_own[1], wqkv[cols, pl.ds(0, width)])
                + dot_nt(c_own[2], wqkv[cols, pl.ds(width, width)])
                + dot_nt(c_own[3], wqkv[cols, pl.ds(2 * width, width)])
            ).astype(BF16)
            return carry

        lax.fori_loop(0, width // otile, dn_tile, 0)
        for s in range(micro):
            h = h_in[sample(s), :].astype(F32)
            r = lax.rsqrt(jnp.mean(h * h, axis=-1, keepdims=True) + 1e-06)
            g = datt[sample(s), :].astype(F32) * (1.0 + mod_part(s, 1))
            dh = r * g - h * (r * r * r) * jnp.mean(g * h, axis=-1, keepdims=True)
            g_send[sample(s), :] = (
                dh.astype(BF16).astype(F32) + g_recv[sample(s), :].astype(F32)
            ).astype(BF16)
        back.start()

    swap_a.wait()
    swap_n.wait()

    def chunk_of(b, rank):
        at = pl.ds(pl.multiple_of(rank * share, share), share)
        own, par = (a_own, a_par) if b == 0 else (n_own, n_par)
        return dot(own[at, :], c_own[b]) + dot(par[at, :], c_par[b])

    def copy_z(b, o):
        return remote(
            z_send.at[b, o - 1], z_recv.at[b, o - 1], zs_sem.at[b, o - 1], zr_sem.at[b, o - 1],
            {"dp": lax.rem(me + 2 * o, ranks)},
        )

    for b in range(4):
        swap_c[b].wait()

        def send_chunk(o, carry, b=b):
            z_send[b, o - 1] = chunk_of(b, lax.rem(me + 2 * o, ranks)).astype(BF16)
            copy_z(b, o).start()
            return carry

        lax.fori_loop(1, half, send_chunk, 0)
    square = jnp.zeros((share, width), F32)
    for b in range(4):
        mine = chunk_of(b, me)

        if b == 0:
            gout_ref[...] = mine
        else:
            gqkv_ref[:, pl.ds((b - 1) * width, width)] = mine
    for b in range(4):
        target = gout_ref if b == 0 else gqkv_ref.at[:, pl.ds((b - 1) * width, width)]

        def add_in(o, carry, b=b, target=target):
            copy_z(b, o).wait()
            target[...] += z_recv[b, o - 1].astype(F32)
            return carry

        lax.fori_loop(1, half, add_in, 0)
        square = square + target[...] * target[...]
    row = jnp.sum(square, axis=0, keepdims=True)
    part = row[:, :128]
    for c in range(1, width // 128):
        part = part + row[:, c * 128 : (c + 1) * 128]
    sq_own[...] = jnp.broadcast_to(part, sq_own.shape)

    def copy_q(o):
        return remote(
            sq_own, sq_recv.at[o - 1], qs_sem.at[o - 1], qr_sem.at[o - 1],
            {"dp": lax.rem(me + o, ranks)},
        )

    def copy_s(o):
        return remote(
            sq_mid, sq_sec.at[o - 1], ss_sem.at[o - 1], sr_sem.at[o - 1],
            {"section": lax.rem(sec + o, sections)},
        )

    def start_with(make):
        def go(o, carry):
            make(o).start()
            return carry

        return go

    def sum_with(make, landed):
        def go(o, total):
            make(o).wait()
            return total + landed[o - 1]

        return go

    lax.fori_loop(1, ranks, start_with(copy_q), 0)
    sq_mid[...] = lax.fori_loop(1, ranks, sum_with(copy_q, sq_recv), sq_own[...])
    lax.fori_loop(1, sections, start_with(copy_s), 0)
    total_ref[...] = lax.fori_loop(1, sections, sum_with(copy_s, sq_sec), sq_mid[...])

    @pl.when(sec < sections - 1)
    def _():
        forward.wait_send()

    @pl.when(sec > 0)
    def _():
        back.wait_send()


def train_step(h0, modulation, noise_pad, head_pad, w_qkv, w_out, sections, ranks):
    rows, width = h0.shape
    micro = modulation.shape[0]
    seq = rows // micro
    half = ranks // 2
    share = width // ranks
    pairs = width // (2 * HEAD_DIM)
    act = pltpu.VMEM((rows, width), BF16)
    turned = pltpu.VMEM((width, rows), BF16)
    vmem = pl.BlockSpec(memory_space=pltpu.VMEM)
    hbm = pl.BlockSpec(memory_space=pl.ANY)
    dma = pltpu.SemaphoreType.DMA
    return pl.pallas_call(
        step_kernel,
        out_shape=(
            jax.ShapeDtypeStruct((share, 3 * width), F32),
            jax.ShapeDtypeStruct((share, width), F32),
            jax.ShapeDtypeStruct((8, 128), F32),
        ),
        in_specs=[vmem, vmem, vmem, vmem, hbm, hbm],
        out_specs=(vmem, vmem, vmem),
        scratch_shapes=[
            pltpu.VMEM(w_qkv.shape, BF16),
            pltpu.VMEM(w_out.shape, BF16),
            act, act, act, act, act, act,
            pltpu.VMEM((rows, 3 * width), BF16),
            act, act,
            pltpu.VMEM((micro * pairs, 2 * seq, seq), F32),
            turned, turned, turned, turned,
            pltpu.VMEM((4, rows, width), BF16),
            pltpu.VMEM((4, rows, width), BF16),
            pltpu.VMEM((4, half - 1, share, width), BF16),
            pltpu.VMEM((4, half - 1, share, width), BF16),
            pltpu.VMEM((8, 128), F32),
            pltpu.VMEM((ranks - 1, 8, 128), F32),
            pltpu.VMEM((8, 128), F32),
            pltpu.VMEM((sections - 1, 8, 128), F32),
            dma((2,)), dma((2,)), dma((2,)), dma((4,)), dma((2, 4)),
            dma((4, half - 1)), dma((4, half - 1)),
            dma((ranks - 1,)), dma((ranks - 1,)),
            dma((sections - 1,)), dma((sections - 1,)),
        ],
        compiler_params=pltpu.CompilerParams(
            collective_id=0, has_side_effects=True, vmem_limit_bytes=60 * 1024 * 1024
        ),
    )(h0, modulation, noise_pad, head_pad, w_qkv, w_out)


def optimizer_step(gradient, moment, second, factor):
    normalized = gradient * factor
    moment_new = 0.9 * moment + 0.1 * normalized
    second_new = 0.99 * second + 0.01 * normalized * normalized
    return (moment_new / (jnp.sqrt(second_new) + 1e-08), moment_new, second_new)


def local(
    latents,
    noise,
    timesteps,
    cameras,
    embed_in,
    camera_table,
    w_mod,
    w_qkv,
    w_out,
    head_out,
    moment_qkv,
    moment_out,
    second_qkv,
    second_out,
):
    sections = lax.axis_size("section")
    ranks = lax.axis_size("dp")
    model_width = w_qkv.shape[1]
    time_emb = time_embed(timesteps, w_mod.shape[1])
    modulation = jnp.dot(time_emb, w_mod[0], preferred_element_type=jnp.float32)
    h0 = jax.vmap(embed_sample, in_axes=(0, 0, 0, 0, None, None))(
        latents, noise, timesteps, cameras, embed_in, camera_table
    ).reshape(-1, model_width)
    channels = noise.shape[1]
    noise_pad = jnp.pad(noise.astype(F32), ((0, 0), (0, 128 - channels), (0, 0)))
    head_pad = jnp.pad(head_out, ((0, 128 - channels), (0, 0)))
    grad_qkv, grad_out, total = train_step(
        h0, modulation, noise_pad, head_pad, w_qkv[0], w_out[0], sections, ranks
    )
    total_sq = jnp.sum(total[0])
    factor = lax.rsqrt(total_sq / (sections * 4 * model_width * model_width) + 1e-12)
    update_qkv, new_moment_qkv, new_second_qkv = optimizer_step(
        grad_qkv[None], moment_qkv, second_qkv, factor
    )
    update_out, new_moment_out, new_second_out = optimizer_step(
        grad_out[None], moment_out, second_out, factor
    )
    return (update_qkv, update_out, new_moment_qkv, new_moment_out, new_second_qkv, new_second_out)


def solution(mesh):
    placed = (
        P("dp", None, None),
        P("dp", None, None),
        P("dp"),
        P("dp", None),
        P(),
        P(),
        P("section", None, None),
        P("section", None, None),
        P("section", None, None),
        P(),
        P("section", "dp", None),
        P("section", "dp", None),
        P("section", "dp", None),
        P("section", "dp", None),
    )
    return jax.shard_map(
        local,
        mesh=mesh,
        in_specs=placed,
        out_specs=(
            P("section", "dp", None),
            P("section", "dp", None),
            P("section", "dp", None),
            P("section", "dp", None),
            P("section", "dp", None),
            P("section", "dp", None),
        ),
        check_vma=False,
    )
```

time: 572 us -> 208 us (0.36); the launches traced: 564 us -> 207 us
  waiting for transfers between devices: 385 us -> 0 us
  Pallas kernels: 0 us -> 192 us
  matrix products: 55.3 us -> 4.05 us
  blocking collectives: 39.3 us -> 0 us
  starting transfers between devices: 22.6 us -> 0 us
  between operations: 20.7 us -> 1.44 us
  local copies, waits for them, and re-layouts: 16.2 us -> 1.55 us
  other arithmetic: 16.5 us -> 8.11 us
  loops' own time: 8.32 us -> 0 us
    reduce_scatter x2 -> x0, waiting for transfers between devices: 291 us -> none  [the longest x1 209 us: local(): lax.psum_scatter(lax.dot_general(normed_all, cot_qkv.reshape(rows_all, 3...]
    pallas_call x0 -> x1, Pallas kernels: none -> 192 us  [train_step(): pl.pallas_call(step_kernel, out_shape=(jax.ShapeDtypeStruct((share, 3 * w...]
    ppermute x8 -> x0, waiting for transfers between devices: 94.1 us -> none  [passed_along(): return lax.ppermute(x, axis, pairs)]
    dot_general x25 -> x0, matrix products: 47.1 us -> none  [the longest x5 17.9 us: piece_a(): jnp.dot(normed, weight_qkv, preferred_element_type=jnp.float32)]
    psum x1 -> x0, blocking collectives: 39.3 us -> none  [local(): total_sq = lax.psum(local_sq, ('section', 'dp'))]
    ppermute x8 -> x0, starting transfers between devices: 22.3 us -> none  [passed_along(): return lax.ppermute(x, axis, pairs)]
    another operation x11 -> x0, loops' own time: 8.32 us -> none  [the longest x4 6.96 us: local(): sent_act, buffers = lax.cond(is_active, active, resting, buffers)]
  transfers between devices with their start and end apart: 10 -> 0, of which waited for: 10 -> 0; matrix products, arithmetic and copies ran while one was open for 2% -> 0% of each run, Pallas kernels for 0% -> 0%
where the time goes in v1:
time: 208 us; the launch traced here: 207 us
  Pallas kernels  192 us (92%)
  other arithmetic  8.11 us (4%)
  matrix products  4.05 us (2%)
    pallas_call x1, Pallas kernels, train_step(): pl.pallas_call(step_kernel, out_shape=(jax.ShapeDtypeStruct((share, 3 * w...  192 us
    div x2, other arithmetic, optimizer_step(): return (moment_new / (jnp.sqrt(second_new) + 1e-08), moment_new, second_new)  6 us

profile of v1, /device:TPU:0, one launch (start us, length us, event | category | flops | bytes accessed | tf_op | source)
XLA Modules:
  0.0 207.5 jit_solution(7865013594850823086)
XLA Ops:
  0.6 0.0 copy-start
  0.6 0.0 copy-start.7
  0.7 1.2 fusion.7
  1.8 0.1 add.54
  2.0 0.7 fusion.19
  2.7 0.0 copy-start.5
  2.7 0.0 copy-start.6
  2.7 1.9 fusion.4
  4.6 0.0 copy-done.7
  4.7 0.1 multiply_cosine_fusion
  4.8 0.0 copy-done
  4.8 0.9 fusion.2.mod_ref
  5.7 0.0 copy-done.5
  5.7 0.7 pad.8.noise_ref
  6.4 0.0 copy-done.6
  6.4 0.7 pad.9.head_ref
  7.1 0.0 copy-start.1
  7.1 192.3 %shard_map.181 = (f32[128,3072]{1,0:T(8,128)}, f32[128,1024]{1,0:T(8,128)}, f32[8,128]{1,0:T(8,128)}) custom-call(bf16[256,1024]{1,0:T(8,128)(2,1)} %bitcast.32, f32[2,3072]{1,0:T(2,128)} %fusion.2.mod_ref, f32[2,128,128]{2,1,0:T(8,128)} %pad.8.noise_ref, bf16[128,1024]{1,0:T(8,128)(2,1)} %pad.9.head_ref, bf16[1024,3072]{1,0:T(8,128)(2,1)} %bitcast.29, ...), custom_call_target="tpu_custom_call" | custom-call | tf_op jit(solution)/shard_map/pallas_call | solution.py:386
  199.5 1.3 slice_reduce_fusion
  201.4 0.0 copy-done.1
  201.4 0.0 copy-start.2
  201.5 0.0 copy-start.3
  201.5 0.0 copy-start.4
  201.5 4.7 %add_divide_fusion = (f32[1,128,3072]{2,1,0:T(8,128)}, f32[1,128,3072]{2,1,0:T(8,128)}, f32[1,128,3072]{2,1,0:T(8,128)}) fusion(f32[128,3072]{1,0:T(8,128)} %get-tuple-element.9, f32[]{:T(128)S(6)} %rsqrt.3, f32[1,128,3072]{2,1,0:T(8,128)S(1)} %copy-done.1, f32[1,128,3072]{2,1,0:T(8,128)} %param.24), kind=kLoop, calls=%fused_computation.6 | loop fusion | flops 3932160 | bytes 9437188 | tf_op jit(solution)/shard_map/div | solution.py:426
  206.2 0.0 copy-done.2
  206.2 0.0 copy-done.3
  206.2 0.0 copy-done.4
  206.2 1.3 add_divide_fusion.1
  (2 shorter events, 0.0 us)
Async XLA Ops:
  0.6 4.1 %copy-start = (bf16[1,256,3072]{2,1,0:T(8,128)(2,1)S(1)}, bf16[1,256,3072]{2,1,0:T(8,128)(2,1)}, u32[]{:S(2)}) copy-start(bf16[1,256,3072]{2,1,0:T(8,128)(2,1)} %param.20) | copy-start | bytes 4718596
  0.6 4.0 %copy-start.7 = (s32[2]{0:T(128)S(1)}, s32[2]{0:T(128)}, u32[]{:S(2)}) copy-start(s32[2]{0:T(128)} %param.16) | copy-start | bytes 28
  2.7 3.0 %copy-start.5 = (bf16[2,4,128]{2,1,0:T(4,128)(2,1)S(1)}, bf16[2,4,128]{2,1,0:T(4,128)(2,1)}, u32[]{:S(2)}) copy-start(bf16[2,4,128]{2,1,0:T(4,128)(2,1)} %param.15) | copy-start | bytes 6148
  2.7 3.7 %copy-start.6 = (bf16[4,1024]{1,0:T(4,128)(2,1)S(1)}, bf16[4,1024]{1,0:T(4,128)(2,1)}, u32[]{:S(2)}) copy-start(bf16[4,1024]{1,0:T(4,128)(2,1)} %param.23) | copy-start | bytes 24580
  7.1 194.3 %copy-start.1 = (f32[1,128,3072]{2,1,0:T(8,128)S(1)}, f32[1,128,3072]{2,1,0:T(8,128)}, u32[]{:S(2)}) copy-start(f32[1,128,3072]{2,1,0:T(8,128)} %param.26) | copy-start | bytes 4718596
  201.4 4.7 %copy-start.2 = (f32[1,128,1024]{2,1,0:T(8,128)S(1)}, f32[1,128,1024]{2,1,0:T(8,128)}, u32[]{:S(2)}) copy-start(f32[1,128,1024]{2,1,0:T(8,128)} %param.27) | copy-start | bytes 1572868
  201.5 4.7 %copy-start.3 = (f32[1,128,1024]{2,1,0:T(8,128)S(1)}, f32[1,128,1024]{2,1,0:T(8,128)}, u32[]{:S(2)}) copy-start(f32[1,128,1024]{2,1,0:T(8,128)} %param.25) | copy-start | bytes 1572868
  201.5 4.7 %copy-start.4 = (f32[128,1024]{1,0:T(8,128)S(1)}, f32[128,1024]{1,0:T(8,128)}, u32[]{:S(2)}) copy-start(f32[128,1024]{1,0:T(8,128)} %get-tuple-element.11) | copy-start | bytes 1572868

commit v2 on v1

--- a/solution.py
+++ b/solution.py
@@ -115,19 +115,28 @@
             device_id=device, device_id_type=MESH,
         )
 
-    forward = remote(
-        h_out, h_recv, fwd_sem.at[0], fwd_sem.at[1],
-        {"section": jnp.minimum(sec + 1, sections - 1)},
-    )
-    back = remote(
-        g_send, g_recv, bwd_sem.at[0], bwd_sem.at[1], {"section": jnp.maximum(sec - 1, 0)}
-    )
+    def forward(s):
+        at = pl.ds(s * seq, seq)
+        return remote(
+            h_out.at[at], h_recv.at[at], fwd_sem.at[0, s], fwd_sem.at[1, s],
+            {"section": jnp.minimum(sec + 1, sections - 1)},
+        )
+
+    def back(s):
+        at = pl.ds(s * seq, seq)
+        return remote(
+            g_send.at[at], g_recv.at[at], bwd_sem.at[0, s], bwd_sem.at[1, s],
+            {"section": jnp.maximum(sec - 1, 0)},
+        )
+
     swap_n = remote(n_own, n_par, t_sem.at[0], t_sem.at[1], {"dp": partner})
     swap_a = remote(a_own, a_par, t_sem.at[2], t_sem.at[3], {"dp": partner})
-    swap_c = [
-        remote(c_own.at[b], c_par.at[b], c_sem.at[0, b], c_sem.at[1, b], {"dp": partner})
-        for b in range(4)
-    ]
+    def swap_c(b, s):
+        at = pl.ds(s * seq, seq)
+        return remote(
+            c_own.at[b, at], c_par.at[b, at], c_sem.at[0, b, s], c_sem.at[1, b, s],
+            {"dp": partner},
+        )
 
     def sample(s):
         return pl.ds(s * seq, seq)
@@ -135,117 +144,117 @@
     def mod_part(s, part):
         return mod_ref[pl.ds(s, 1), pl.ds(part * width, width)]
 
-    @pl.when(sec == 0)
-    def _():
-        h_in[...] = h0_ref[...]
-
-    @pl.when(sec > 0)
-    def _():
-        forward.wait_recv()
-        h_in[...] = h_recv[...]
-
-    for s in range(micro):
-        h = h_in[sample(s), :].astype(F32)
-        mean_sq = jnp.mean(h * h, axis=-1, keepdims=True)
-        nrm[sample(s), :] = (
-            h * lax.rsqrt(mean_sq + 1e-06) * (1.0 + mod_part(s, 1)) + mod_part(s, 0)
-        ).astype(BF16)
-    load_qkv.wait()
     tile = width // 2
-
-    def qkv_tile(t, carry):
-        cols = pl.ds(pl.multiple_of(t * tile, tile), tile)
-        qkv[:, cols] = dot(nrm[...], wqkv[:, cols]).astype(BF16)
-        return carry
-
-    lax.fori_loop(0, 3 * width // tile, qkv_tile, 0)
+    otile = width // 4
 
     def heads_at(j, part):
         start = part * width + j * 2 * HEAD_DIM
         return pl.ds(pl.multiple_of(start, 2 * HEAD_DIM), 2 * HEAD_DIM)
 
-    def attend(j, carry):
-        masks = lane_masks()
-        for s in range(micro):
-            q2 = stacked(qkv[sample(s), heads_at(j, 0)], masks)
-            k = qkv[sample(s), heads_at(j, 1)]
-            v2 = stacked(qkv[sample(s), heads_at(j, 2)], masks)
+    def layer_forward(s):
+        here = sample(s)
+
+        @pl.when(sec == 0)
+        def _():
+            h_in[here, :] = h0_ref[here, :]
+
+        @pl.when(sec > 0)
+        def _():
+            forward(s).wait_recv()
+            h_in[here, :] = h_recv[here, :]
+
+        h = h_in[here, :].astype(F32)
+        mean_sq = jnp.mean(h * h, axis=-1, keepdims=True)
+        nrm[here, :] = (
+            h * lax.rsqrt(mean_sq + 1e-06) * (1.0 + mod_part(s, 1)) + mod_part(s, 0)
+        ).astype(BF16)
+        if s == 0:
+            load_qkv.wait()
+
+        def qkv_tile(t, carry):
+            cols = pl.ds(pl.multiple_of(t * tile, tile), tile)
+            qkv[here, cols] = dot(nrm[here, :], wqkv[:, cols]).astype(BF16)
+            return carry
+
+        lax.fori_loop(0, 3 * width // tile, qkv_tile, 0)
+
+        def attend(j, carry):
+            masks = lane_masks()
+            q2 = stacked(qkv[here, heads_at(j, 0)], masks)
+            k = qkv[here, heads_at(j, 1)]
+            v2 = stacked(qkv[here, heads_at(j, 2)], masks)
             scores = dot_nt(q2, k) * (1.0 / math.sqrt(HEAD_DIM))
             e = jnp.exp(scores - jnp.max(scores, axis=-1, keepdims=True))
             p = e / jnp.sum(e, axis=-1, keepdims=True)
             probs[s * pairs + j] = p
             p2 = p.astype(BF16)
             wide = jnp.concatenate([p2[:seq], p2[seq:]], axis=1)
-            att[sample(s), heads_at(j, 0)] = dot(wide, v2).astype(BF16)
-        return carry
-
-    lax.fori_loop(0, pairs, attend, 0, unroll=2)
-    load_out.wait()
-    otile = width // 4
-
-    def out_tile(t, carry):
-        cols = pl.ds(pl.multiple_of(t * otile, otile), otile)
-        projected = dot(att[...], wout[:, cols])
-        for s in range(micro):
+            att[here, heads_at(j, 0)] = dot(wide, v2).astype(BF16)
+            return carry
+
+        lax.fori_loop(0, pairs, attend, 0, unroll=4)
+        if s == 0:
+            load_out.wait()
+
+        def out_tile(t, carry):
+            cols = pl.ds(pl.multiple_of(t * otile, otile), otile)
             gate = mod_ref[pl.ds(s, 1), pl.ds(pl.multiple_of(2 * width + t * otile, otile), otile)]
-            h = h_in[sample(s), cols].astype(F32)
-            h_out[sample(s), cols] = (
-                h + gate * projected[s * seq : (s + 1) * seq]
+            h_out[here, cols] = (
+                h_in[here, cols].astype(F32) + gate * dot(att[here, :], wout[:, cols])
             ).astype(BF16)
-        return carry
-
-    lax.fori_loop(0, width // otile, out_tile, 0)
-
-    @pl.when(sec < sections - 1)
-    def _():
-        forward.start()
-
-    def turn(t, carry):
-        cols = pl.ds(pl.multiple_of(t * otile, otile), otile)
-        n_own[cols, :] = nrm[:, cols].T
-        a_own[cols, :] = att[:, cols].T
-        return carry
-
-    lax.fori_loop(0, width // otile, turn, 0)
-    swap_n.start()
-    swap_a.start()
-
-    @pl.when(sec == sections - 1)
-    def _():
-        for s in range(micro):
-            h = h_out[sample(s), :].astype(F32)
+            return carry
+
+        lax.fori_loop(0, width // otile, out_tile, 0)
+
+        @pl.when(sec < sections - 1)
+        def _():
+            forward(s).start()
+
+    def swap_turned():
+        def turn(t, carry):
+            cols = pl.ds(pl.multiple_of(t * otile, otile), otile)
+            n_own[cols, :] = nrm[:, cols].T
+            a_own[cols, :] = att[:, cols].T
+            return carry
+
+        lax.fori_loop(0, width // otile, turn, 0)
+        swap_n.start()
+        swap_a.start()
+
+    def layer_backward(s):
+        here = sample(s)
+
+        @pl.when(sec == sections - 1)
+        def _():
+            h = h_out[here, :].astype(F32)
             r = lax.rsqrt(jnp.mean(h * h, axis=-1, keepdims=True) + 1e-06)
             n = (h * r).astype(BF16)
             predicted = dot_nt(head_ref[...], n)
             err = 2.0 * (predicted - noise_ref[s])
             dn = dot(err.T.astype(BF16), head_ref[...]).astype(BF16).astype(F32)
             dh = r * dn - h * (r * r * r) * jnp.mean(dn * h, axis=-1, keepdims=True)
-            g_recv[sample(s), :] = dh.astype(BF16)
-
-    @pl.when(sec < sections - 1)
-    def _():
-        back.wait_recv()
-
-    for s in range(micro):
-        c_own[0, sample(s), :] = (
-            mod_part(s, 2) * g_recv[sample(s), :].astype(F32)
-        ).astype(BF16)
-    swap_c[0].start()
-
-    def datt_tile(t, carry):
-        cols = pl.ds(pl.multiple_of(t * otile, otile), otile)
-        datt[:, cols] = dot_nt(c_own[0], wout[cols, :]).astype(BF16)
-        return carry
-
-    lax.fori_loop(0, width // otile, datt_tile, 0)
-
-    def attend_back(j, carry):
-        masks = lane_masks()
-        for s in range(micro):
-            q2 = stacked(qkv[sample(s), heads_at(j, 0)], masks)
-            k2 = stacked(qkv[sample(s), heads_at(j, 1)], masks)
-            v = qkv[sample(s), heads_at(j, 2)]
-            da2 = stacked(datt[sample(s), heads_at(j, 0)], masks)
+            g_recv[here, :] = dh.astype(BF16)
+
+        @pl.when(sec < sections - 1)
+        def _():
+            back(s).wait_recv()
+
+        c_own[0, here, :] = (mod_part(s, 2) * g_recv[here, :].astype(F32)).astype(BF16)
+
+        def datt_tile(t, carry):
+            cols = pl.ds(pl.multiple_of(t * otile, otile), otile)
+            datt[here, cols] = dot_nt(c_own[0, here, :], wout[cols, :]).astype(BF16)
+            return carry
+
+        lax.fori_loop(0, width // otile, datt_tile, 0)
+        swap_c(0, s).start()
+
+        def attend_back(j, carry):
+            masks = lane_masks()
+            q2 = stacked(qkv[here, heads_at(j, 0)], masks)
+            k2 = stacked(qkv[here, heads_at(j, 1)], masks)
+            v = qkv[here, heads_at(j, 2)]
+            da2 = stacked(datt[here, heads_at(j, 0)], masks)
             p = probs[s * pairs + j]
             dp = dot_nt(da2, v).astype(BF16).astype(F32)
             ds = (p * (dp - jnp.sum(dp * p, axis=-1, keepdims=True))) * (
@@ -253,36 +262,49 @@
             )
             db = ds.astype(BF16)
             wide = jnp.concatenate([db[:seq], db[seq:]], axis=1)
-            c_own[1, sample(s), heads_at(j, 0)] = dot(wide, k2).astype(BF16)
-            c_own[2, sample(s), heads_at(j, 0)] = dot(ds.T.astype(BF16), q2).astype(BF16)
-            c_own[3, sample(s), heads_at(j, 0)] = dot(p.T.astype(BF16), da2).astype(BF16)
-        return carry
-
-    lax.fori_loop(0, pairs, attend_back, 0, unroll=2)
-    for b in range(1, 4):
-        swap_c[b].start()
-
-    @pl.when(sec > 0)
+            c_own[1, here, heads_at(j, 0)] = dot(wide, k2).astype(BF16)
+            c_own[2, here, heads_at(j, 0)] = dot(ds.T.astype(BF16), q2).astype(BF16)
+            c_own[3, here, heads_at(j, 0)] = dot(p.T.astype(BF16), da2).astype(BF16)
+            return carry
+
+        lax.fori_loop(0, pairs, attend_back, 0, unroll=4)
+        for b in range(1, 4):
+            swap_c(b, s).start()
+
+        @pl.when(sec > 0)
+        def _():
+            def dn_tile(t, carry):
+                cols = pl.ds(pl.multiple_of(t * otile, otile), otile)
+                datt[here, cols] = (
+                    dot_nt(c_own[1, here, :], wqkv[cols, pl.ds(0, width)])
+                    + dot_nt(c_own[2, here, :], wqkv[cols, pl.ds(width, width)])
+                    + dot_nt(c_own[3, here, :], wqkv[cols, pl.ds(2 * width, width)])
+                ).astype(BF16)
+                return carry
+
+            lax.fori_loop(0, width // otile, dn_tile, 0)
+            h = h_in[here, :].astype(F32)
+            r = lax.rsqrt(jnp.mean(h * h, axis=-1, keepdims=True) + 1e-06)
+            g = datt[here, :].astype(F32) * (1.0 + mod_part(s, 1))
+            dh = r * g - h * (r * r * r) * jnp.mean(g * h, axis=-1, keepdims=True)
+            g_send[here, :] = (
+                dh.astype(BF16).astype(F32) + g_recv[here, :].astype(F32)
+            ).astype(BF16)
+            back(s).start()
+
+    for s in range(micro):
+        layer_forward(s)
+
+    @pl.when(sec < sections - 1)
     def _():
-        def dn_tile(t, carry):
-            cols = pl.ds(pl.multiple_of(t * otile, otile), otile)
-            datt[:, cols] = (
-                dot_nt(c_own[1], wqkv[cols, pl.ds(0, width)])
-                + dot_nt(c_own[2], wqkv[cols, pl.ds(width, width)])
-                + dot_nt(c_own[3], wqkv[cols, pl.ds(2 * width, width)])
-            ).astype(BF16)
-            return carry
-
-        lax.fori_loop(0, width // otile, dn_tile, 0)
-        for s in range(micro):
-            h = h_in[sample(s), :].astype(F32)
-            r = lax.rsqrt(jnp.mean(h * h, axis=-1, keepdims=True) + 1e-06)
-            g = datt[sample(s), :].astype(F32) * (1.0 + mod_part(s, 1))
-            dh = r * g - h * (r * r * r) * jnp.mean(g * h, axis=-1, keepdims=True)
-            g_send[sample(s), :] = (
-                dh.astype(BF16).astype(F32) + g_recv[sample(s), :].astype(F32)
-            ).astype(BF16)
-        back.start()
+        swap_turned()
+
+    for s in range(micro):
+        layer_backward(s)
+
+    @pl.when(sec == sections - 1)
+    def _():
+        swap_turned()
 
     swap_a.wait()
     swap_n.wait()
@@ -299,7 +321,8 @@
         )
 
     for b in range(4):
-        swap_c[b].wait()
+        for s in range(micro):
+            swap_c(b, s).wait()
 
         def send_chunk(o, carry, b=b):
             z_send[b, o - 1] = chunk_of(b, lax.rem(me + 2 * o, ranks)).astype(BF16)
@@ -364,11 +387,13 @@
 
     @pl.when(sec < sections - 1)
     def _():
-        forward.wait_send()
+        for s in range(micro):
+            forward(s).wait_send()
 
     @pl.when(sec > 0)
     def _():
-        back.wait_send()
+        for s in range(micro):
+            back(s).wait_send()
 
 
 def train_step(h0, modulation, noise_pad, head_pad, w_qkv, w_out, sections, ranks):
@@ -408,7 +433,7 @@
             pltpu.VMEM((ranks - 1, 8, 128), F32),
             pltpu.VMEM((8, 128), F32),
             pltpu.VMEM((sections - 1, 8, 128), F32),
-            dma((2,)), dma((2,)), dma((2,)), dma((4,)), dma((2, 4)),
+            dma((2,)), dma((2, micro)), dma((2, micro)), dma((4,)), dma((2, 4, micro)),
             dma((4, half - 1)), dma((4, half - 1)),
             dma((ranks - 1,)), dma((ranks - 1,)),
             dma((sections - 1,)), dma((sections - 1,)),

time: 208 us -> 200 us (0.962)
  Pallas kernels: 192 us -> 184 us
    pallas_call x1, Pallas kernels: 192 us -> 184 us  [train_step(): pl.pallas_call(step_kernel, out_shape=(jax.ShapeDtypeStruct((share, 3 * w...]
where the time goes in v2:
time: 200 us; the launch traced here: 199 us
  Pallas kernels  184 us (92%)
  other arithmetic  8.11 us (4%)
  matrix products  4.05 us (2%)
    pallas_call x1, Pallas kernels, train_step(): pl.pallas_call(step_kernel, out_shape=(jax.ShapeDtypeStruct((share, 3 * w...  184 us
    div x2, other arithmetic, optimizer_step(): return (moment_new / (jnp.sqrt(second_new) + 1e-08), moment_new, second_new)  6 us

profile of v2, /device:TPU:0, one launch (start us, length us, event | category | flops | bytes accessed | tf_op | source)
XLA Modules:
  0.0 199.4 jit_solution(14024352739293317711)
XLA Ops:
  0.6 0.0 copy-start
  0.6 0.0 copy-start.7
  0.7 1.2 fusion.7
  1.8 0.1 add.54
  2.0 0.7 fusion.19
  2.7 0.0 copy-start.5
  2.7 0.0 copy-start.6
  2.7 1.9 fusion.4
  4.6 0.0 copy-done.7
  4.7 0.1 multiply_cosine_fusion
  4.8 0.0 copy-done
  4.8 0.9 fusion.2.mod_ref
  5.7 0.0 copy-done.5
  5.7 0.7 pad.8.noise_ref
  6.4 0.0 copy-done.6
  6.4 0.7 pad.9.head_ref
  7.1 0.0 copy-start.1
  7.1 184.3 %shard_map.181 = (f32[128,3072]{1,0:T(8,128)}, f32[128,1024]{1,0:T(8,128)}, f32[8,128]{1,0:T(8,128)}) custom-call(bf16[256,1024]{1,0:T(8,128)(2,1)} %bitcast.32, f32[2,3072]{1,0:T(2,128)} %fusion.2.mod_ref, f32[2,128,128]{2,1,0:T(8,128)} %pad.8.noise_ref, bf16[128,1024]{1,0:T(8,128)(2,1)} %pad.9.head_ref, bf16[1024,3072]{1,0:T(8,128)(2,1)} %bitcast.29, ...), custom_call_target="tpu_custom_call" | custom-call | tf_op jit(solution)/shard_map/pallas_call | solution.py:411
  191.4 1.3 slice_reduce_fusion
  193.3 0.0 copy-done.1
  193.4 0.0 copy-start.2
  193.4 0.0 copy-start.3
  193.4 0.0 copy-start.4
  193.4 4.7 %add_divide_fusion = (f32[1,128,3072]{2,1,0:T(8,128)}, f32[1,128,3072]{2,1,0:T(8,128)}, f32[1,128,3072]{2,1,0:T(8,128)}) fusion(f32[128,3072]{1,0:T(8,128)} %get-tuple-element.9, f32[]{:T(128)S(6)} %rsqrt.3, f32[1,128,3072]{2,1,0:T(8,128)S(1)} %copy-done.1, f32[1,128,3072]{2,1,0:T(8,128)} %param.24), kind=kLoop, calls=%fused_computation.6 | loop fusion | flops 3932160 | bytes 9437188 | tf_op jit(solution)/shard_map/div | solution.py:451
  198.1 0.0 copy-done.2
  198.1 0.0 copy-done.3
  198.1 0.0 copy-done.4
  198.1 1.3 add_divide_fusion.1
  (2 shorter events, 0.0 us)
Async XLA Ops:
  0.6 4.1 %copy-start = (bf16[1,256,3072]{2,1,0:T(8,128)(2,1)S(1)}, bf16[1,256,3072]{2,1,0:T(8,128)(2,1)}, u32[]{:S(2)}) copy-start(bf16[1,256,3072]{2,1,0:T(8,128)(2,1)} %param.20) | copy-start | bytes 4718596
  0.6 4.0 %copy-start.7 = (s32[2]{0:T(128)S(1)}, s32[2]{0:T(128)}, u32[]{:S(2)}) copy-start(s32[2]{0:T(128)} %param.16) | copy-start | bytes 28
  2.7 3.0 %copy-start.5 = (bf16[2,4,128]{2,1,0:T(4,128)(2,1)S(1)}, bf16[2,4,128]{2,1,0:T(4,128)(2,1)}, u32[]{:S(2)}) copy-start(bf16[2,4,128]{2,1,0:T(4,128)(2,1)} %param.15) | copy-start | bytes 6148
  2.7 3.7 %copy-start.6 = (bf16[4,1024]{1,0:T(4,128)(2,1)S(1)}, bf16[4,1024]{1,0:T(4,128)(2,1)}, u32[]{:S(2)}) copy-start(bf16[4,1024]{1,0:T(4,128)(2,1)} %param.23) | copy-start | bytes 24580
  7.1 186.2 %copy-start.1 = (f32[1,128,3072]{2,1,0:T(8,128)S(1)}, f32[1,128,3072]{2,1,0:T(8,128)}, u32[]{:S(2)}) copy-start(f32[1,128,3072]{2,1,0:T(8,128)} %param.26) | copy-start | bytes 4718596
  193.4 4.7 %copy-start.2 = (f32[1,128,1024]{2,1,0:T(8,128)S(1)}, f32[1,128,1024]{2,1,0:T(8,128)}, u32[]{:S(2)}) copy-start(f32[1,128,1024]{2,1,0:T(8,128)} %param.27) | copy-start | bytes 1572868
  193.4 4.7 %copy-start.3 = (f32[1,128,1024]{2,1,0:T(8,128)S(1)}, f32[1,128,1024]{2,1,0:T(8,128)}, u32[]{:S(2)}) copy-start(f32[1,128,1024]{2,1,0:T(8,128)} %param.25) | copy-start | bytes 1572868
  193.4 4.7 %copy-start.4 = (f32[128,1024]{1,0:T(8,128)S(1)}, f32[128,1024]{1,0:T(8,128)}, u32[]{:S(2)}) copy-start(f32[128,1024]{1,0:T(8,128)} %get-tuple-element.11) | copy-start | bytes 1572868
